TPU v7x, 32 devices: a whole 2x2x4 slice. The times are simulated.
32 devices in a mesh: dp: 16 (over z, x, core), mp: 2 (over y).
Axes of the slice: x: 2, y: 2, z: 4, core: 2. Of those that a mesh axis runs over, the one named last changes fastest.
Arguments:
- tokens: bfloat16 [8192, 8192], P('dp'), may hold values from -6 to 6
- queries: bfloat16 [8192, 64, 128], P('dp', 'mp'), may hold values from -68 to 68
- out_grad: bfloat16 [8192, 64, 128], P('dp', 'mp'), may hold values from -6 to 6
- segment_ids: int32 [16, 512], P('dp'), may hold values from 0 to 3, never falling along the last dimension, each value on 1 to 256 neighbouring positions
- weight_slots: bfloat16 [16384, 8, 2, 128], P('dp', 'mp'), may hold values from -0.0625 to 0.0625
- old_place: int32 [64], replicated, may hold values from 0 to 127, as said below
- new_place: int32 [64], replicated, may hold values from 0 to 127, as said below
Outputs:
- input_grad: bfloat16 [8192, 8192], P('dp', 'mp')
- query_grad: bfloat16 [8192, 64, 128], P('dp', 'mp')
- weight_grad: float32 [16384, 8, 2, 128], P('dp', 'mp')
Inputs may be any that keep to these rules, and one draw needn't show every extreme that they name: `old_place`: entries are distinct slot numbers; slot s lies on index s // 8 of dp; some index of dp holds 8 blocks. `new_place`: entries are distinct slot numbers; slot s lies on index s // 8 of dp; some index of dp receives 8 blocks.
All inputs are finite; a program needn't handle non-finite values.
Results may differ from a plain program's by a relative error of at most 0.018.
Values may be sent and summed in bfloat16 or wider, within the bound.
A program may use at most 192 MiB of HBM per device.

v0:
```python
import jax
import jax.numpy as jnp
from jax import lax
from jax.sharding import PartitionSpec as P

BR = 128


def attend(tokens, weights, queries, out_grad, seg_row):
    tok_count = tokens.shape[0]
    model_width = weights.shape[0]
    head_count = weights.shape[1]
    head_size = weights.shape[3]
    per_head = queries.shape[1] // head_count
    half_size = head_size // 2
    projected = jnp.dot(
        tokens,
        weights.reshape(model_width, head_count * 2 * head_size),
        preferred_element_type=jnp.float32,
    )
    projected = projected.reshape(tok_count, head_count, 2, head_size)
    frequency = 500000.0 ** (-2.0 * jnp.arange(half_size, dtype=jnp.float32) / head_size)
    angle_tab = jnp.arange(tok_count, dtype=jnp.float32)[:, None] * frequency[None, :]
    cos_tab = jnp.cos(angle_tab)[:, None, :]
    sin_tab = jnp.sin(angle_tab)[:, None, :]
    lower_half = projected[:, :, 0, :half_size]
    upper_half = projected[:, :, 0, half_size:]
    rot_keys = jnp.concatenate(
        [lower_half * cos_tab - upper_half * sin_tab, upper_half * cos_tab + lower_half * sin_tab],
        axis=-1,
    ).astype(jnp.bfloat16)
    values = projected[:, :, 1].astype(jnp.bfloat16)
    inv_root = 1.0 / jnp.sqrt(jnp.float32(head_size))
    query_wide = queries.reshape(tok_count, head_count, per_head, head_size).astype(jnp.float32)
    outgrad_wide = out_grad.reshape(tok_count, head_count, per_head, head_size).astype(jnp.float32)
    key_wide = rot_keys.astype(jnp.float32)
    value_wide = values.astype(jnp.float32)
    scores = jnp.einsum("qhgd,khd->hgqk", query_wide, key_wide) * inv_root
    position = jnp.arange(tok_count)
    allowed = (position[:, None] >= position[None, :]) & (seg_row[:, None] == seg_row[None, :])
    scores = jnp.where(allowed, scores, jnp.float32(-1e30))
    row_max = jnp.max(scores, axis=-1, keepdims=True)
    exp_scores = jnp.exp(scores - row_max)
    attn_prob = exp_scores / jnp.sum(exp_scores, axis=-1, keepdims=True)
    prob_half = lax.optimization_barrier(attn_prob.astype(jnp.bfloat16)).astype(jnp.float32)
    attn_out = jnp.einsum("hgqk,khd->qhgd", prob_half, value_wide)
    row_dot = jnp.sum(outgrad_wide * attn_out, axis=-1)
    prob_grad = jnp.einsum("qhgd,khd->hgqk", outgrad_wide, value_wide)
    score_grad = attn_prob * (prob_grad - jnp.transpose(row_dot, (1, 2, 0))[..., None])
    score_half = lax.optimization_barrier(score_grad.astype(jnp.bfloat16)).astype(jnp.float32)
    query_grad = (
        (jnp.einsum("hgqk,khd->qhgd", score_half, key_wide) * inv_root)
        .reshape(tok_count, head_count * per_head, head_size)
        .astype(jnp.bfloat16)
    )
    rot_grad = jnp.einsum("hgqk,qhgd->khd", score_half, query_wide) * inv_root
    value_grad = jnp.einsum("hgqk,qhgd->khd", prob_half, outgrad_wide)
    grad_lower = rot_grad[..., :half_size]
    grad_upper = rot_grad[..., half_size:]
    key_grad = jnp.concatenate(
        [grad_lower * cos_tab + grad_upper * sin_tab, grad_upper * cos_tab - grad_lower * sin_tab],
        axis=-1,
    )
    pair_grad = jnp.stack([key_grad, value_grad], axis=2).astype(jnp.bfloat16)
    return (query_grad, pair_grad)


def pick_blocks(selector, source, block_rows):
    block_total = source.shape[0] // block_rows
    flat = source.reshape(block_total, -1)
    picked = jnp.dot(selector.astype(jnp.bfloat16), flat, preferred_element_type=jnp.float32)
    return picked


def local(tokens, queries, out_grad, segment_ids, weight_slots, old_place, new_place):
    tok_count = tokens.shape[0]
    slot_rows = weight_slots.shape[0]
    head_count = weight_slots.shape[1]
    head_size = weight_slots.shape[3]
    block_rows = BR
    slot_count = slot_rows // block_rows
    dp_count = lax.axis_size("dp")
    slot_total = dp_count * slot_count
    block_count = old_place.shape[0]
    gathered = lax.all_gather(weight_slots, "dp", axis=0, tiled=True)
    all_slots = jnp.arange(slot_total, dtype=jnp.int32)
    old_pick = (old_place[:, None] == all_slots[None, :]).astype(jnp.int32)
    weights = pick_blocks(old_pick, gathered, block_rows).astype(jnp.bfloat16)
    weights = weights.reshape(block_count * block_rows, head_count, 2, head_size)
    query_grad, pair_grad = attend(tokens, weights, queries, out_grad, segment_ids[0])
    pair_flat = pair_grad.reshape(tok_count, head_count * 2 * head_size)
    seq_part = lax.dot_general(
        tokens, pair_flat, (((0,), (0,)), ((), ())), preferred_element_type=jnp.float32
    ).astype(jnp.bfloat16)
    slot_ids = jnp.arange(slot_total, dtype=jnp.int32)
    matched = (new_place[None, :] == slot_ids[:, None]).astype(jnp.bfloat16)
    part_blocks = seq_part.reshape(block_count, -1)
    term = jnp.dot(matched, part_blocks, preferred_element_type=jnp.float32)
    weight_grad = lax.psum_scatter(
        term.reshape(slot_rows * lax.axis_size("dp"), head_count * 2 * head_size).astype(
            jnp.bfloat16
        ),
        "dp",
        scatter_dimension=0,
        tiled=True,
    ).astype(jnp.float32)
    all_heads = lax.all_gather(pair_grad, "mp", axis=1, tiled=True)
    rows_all = lax.all_to_all(weights, "mp", split_axis=0, concat_axis=1, tiled=True)
    heads_flat = all_heads.reshape(tok_count, -1)
    rows_flat = rows_all.reshape(rows_all.shape[0], -1)
    input_grad = lax.dot_general(
        heads_flat, rows_flat, (((1,), (1,)), ((), ())), preferred_element_type=jnp.float32
    ).astype(jnp.bfloat16)
    return (input_grad, query_grad, weight_grad.reshape(slot_rows, head_count, 2, head_size))


def solution(mesh):
    return jax.shard_map(
        local,
        mesh=mesh,
        in_specs=(
            P("dp", None),
            P("dp", "mp", None),
            P("dp", "mp", None),
            P("dp", None),
            P("dp", "mp", None, None),
            P(),
            P(),
        ),
        out_specs=(P("dp", "mp"), P("dp", "mp", None), P("dp", "mp", None, None)),
        check_vma=False,
    )
```

profile of v0, /device:TPU:0, one launch (start us, length us, event | category | flops | bytes accessed | tf_op | source)
XLA Modules:
  0.0 885.2 jit_solution(16510195528750602497)
XLA Ops:
  27.3 154.5 %all-gather.3.cloned.1.call-done = bf16[16384,4,2,128]{3,1,2,0:T(4,128)(2,1)} async-done(((bf16[1024,4,2,128]{3,1,2,0:T(4,128)(2,1)}), bf16[16384,4,2,128]{3,1,2,0:T(4,128)(2,1)}) %all-gather.3.cloned.1.call-update) | async-done | bytes 33554448 | tf_op jit(solution)/shard_map/all_gather | solution.py:85
  181.8 64.4 %copy.89 = bf16[16384,4,2,128]{3,2,1,0:T(2,128)(2,1)} copy(bf16[16384,4,2,128]{3,1,2,0:T(4,128)(2,1)} %all-gather.3.cloned.1.call-done) | data formatting | bytes 67108864 | tf_op jit(solution)/shard_map/all_gather | solution.py:85
  246.2 34.5 %reshape.90 = bf16[128,131072]{1,0:T(8,128)(2,1)} reshape(bf16[16384,4,2,128]{3,2,1,0:T(2,128)(2,1)} %copy.89) | data formatting | bytes 67108864 | tf_op jit(solution)/shard_map/reshape | solution.py:70
  280.7 18.9 %convolution_convert_fusion.1 = bf16[64,131072]{1,0:T(8,128)(2,1)} fusion(bf16[128,131072]{1,0:T(8,128)(2,1)} %reshape.90, s32[64]{0:T(128)S(1)} %copy-done.6), kind=kOutput, calls=%fused_computation.2 | convolution fusion | flops 2155896832 | bytes 50331904 | tf_op jit(solution)/shard_map/dot_general | solution.py:71
  299.6 17.0 %reshape_reshape.3 = bf16[8192,1024]{1,0:T(8,128)(2,1)} reshape(bf16[64,131072]{1,0:T(8,128)(2,1)} %convolution_convert_fusion.1) | data formatting | bytes 33554432 | tf_op jit(solution)/shard_map/reshape;reshape | solution.py:18
  316.6 14.3 %fusion.31 = f32[1024,512]{1,0:T(8,128)S(1)} fusion(bf16[8192,1024]{1,0:T(8,128)(2,1)} %reshape_reshape.3, bf16[512,8192]{1,0:T(8,128)(2,1)} %param.7), kind=kOutput, calls=%fused_computation.57 | convolution fusion | flops 8589934592 | bytes 27262976 | tf_op jit(solution)/shard_map/dot_general | solution.py:16
  335.9 20.5 %fusion.30 = (f32[4,8,512]{2,1,0:T(8,128)S(1)}, f32[4,8,512,512]{2,3,1,0:T(8,128)}) fusion(pred[512,512]{0,1:T(8,128)(4,1)S(1)} %fusion.18, bf16[512,4,8,128]{0,3,2,1:T(8,128)(2,1)} %copy.99, bf16[512,4,64]{2,0,1:T(8,128)(2,1)} %get-tuple-element.19, bf16[512,4,64]{2,0,1:T(8,128)(2,1)} %get-tuple-element.18), kind=kOutput, calls=%fused_computation.56 | convolution fusion | flops 2182087168 | bytes 38600704 | tf_op jit(solution)/shard_map/sub | solution.py:43
  356.3 18.1 %fusion.7 = bf16[4,8,512,512]{2,3,1,0:T(8,128)(2,1)} fusion(f32[4,8,512,512]{2,3,1,0:T(8,128)} %get-tuple-element.27, f32[4,8,512]{2,1,0:T(8,128)S(1)} %get-tuple-element.26), kind=kLoop, calls=%fused_computation.14 | loop fusion | flops 16777216 | bytes 50397184 | tf_op jit(solution)/shard_map/convert_element_type | solution.py:45
  374.4 8.9 %convolution_bitcast_fusion = bf16[512,4,1,128]{3,0,1,2:T(8,128)(2,1)} fusion(bf16[4,8,512,512]{2,3,1,0:T(8,128)(2,1)} %fusion.7, bf16[512,4,8,128]{0,3,2,1:T(8,128)(2,1)S(1)} %bitcast.120), kind=kOutput, calls=%fused_computation.22 | convolution fusion | flops 2147483648 | bytes 21495808 | tf_op jit(solution)/shard_map/hgqk,qhgd->khd/dot_general | solution.py:57
  392.0 25.1 %fusion.2 = bf16[4,8,512,512]{2,3,1,0:T(8,128)(2,1)} fusion(f32[4,8,512]{2,1,0:T(8,128)S(1)} %bitcast.129, f32[4,8,512,512]{2,3,1,0:T(8,128)} %get-tuple-element.27, f32[4,8,512]{2,1,0:T(8,128)S(1)} %get-tuple-element.26, bf16[512,4,8,128]{3,2,1,0:T(8,128)(2,1)} %bitcast.124, bf16[512,4,1,128]{3,0,1,2:T(8,128)(2,1)} %copy.132), kind=kOutput, calls=%fused_computation.5 | convolution fusion | flops 2181038080 | bytes 55181312 | tf_op jit(solution)/shard_map/qhgd,khd->hgqk/dot_general | solution.py:48
  417.1 9.4 %fusion.13 = f32[512,4,128]{2,0,1:T(8,128)S(1)} fusion(bf16[4,8,512,512]{2,3,1,0:T(8,128)(2,1)} %fusion.2, bf16[512,4,8,128]{0,3,2,1:T(8,128)(2,1)} %copy.99), kind=kOutput, calls=%fused_computation.25 | convolution fusion | flops 2147745792 | bytes 22020096 | tf_op jit(solution)/shard_map/hgqk,qhgd->khd/dot_general | solution.py:56
  430.1 15.1 %convert_bitcast_fusion = bf16[8192,1024]{0,1:T(8,128)(2,1)} fusion(bf16[512,1024]{0,1:T(8,128)(2,1)S(1)} %bitcast.128, bf16[512,8192]{1,0:T(8,128)(2,1)} %param.7), kind=kOutput, calls=%fused_computation.9 | convolution fusion | flops 8598323200 | bytes 26214400 | tf_op jit(solution)/shard_map/dot_general | solution.py:92
  445.2 22.4 %copy.109 = bf16[8192,1024]{1,0:T(8,128)(2,1)} copy(bf16[8192,1024]{0,1:T(8,128)(2,1)} %convert_bitcast_fusion) | data formatting | bytes 33554432 | tf_op jit(solution)/shard_map/convert_element_type | solution.py:94
  467.6 17.0 %reshape.97 = bf16[64,131072]{1,0:T(8,128)(2,1)} reshape(bf16[8192,1024]{1,0:T(8,128)(2,1)} %copy.109) | data formatting | bytes 33554432 | tf_op jit(solution)/shard_map/reshape | solution.py:97
  484.6 23.0 %convolution_convert_fusion = bf16[128,131072]{1,0:T(8,128)(2,1)} fusion(bf16[64,131072]{1,0:T(8,128)(2,1)} %reshape.97, s32[64]{0:T(128)S(1)} %copy-done.5), kind=kOutput, calls=%fused_computation.1 | convolution fusion | flops 2164269056 | bytes 50331904 | tf_op jit(solution)/shard_map/dot_general | solution.py:98
  507.6 33.2 %convert_element_type.77 = bf16[16384,1024]{1,0:T(8,128)(2,1)} reshape(bf16[128,131072]{1,0:T(8,128)(2,1)} %convolution_convert_fusion) | data formatting | bytes 67108864 | tf_op jit(solution)/shard_map/convert_element_type | solution.py:100
  540.9 21.3 %reshape.95 = bf16[8192,4,2,128]{3,2,1,0:T(2,128)(2,1)} reshape(bf16[64,131072]{1,0:T(8,128)(2,1)} %convolution_convert_fusion.1) | data formatting | bytes 33554432 | tf_op jit(solution)/shard_map/reshape | solution.py:89
  562.2 12.9 %all-to-all-start = ((bf16[8192,4,2,128]{3,2,1,0:T(2,128)(2,1)}), bf16[8192,4,2,128]{3,2,1,0:T(2,128)(2,1)}, u32[]{:S(2)}, u32[]{:S(2)}) async-start(bf16[8192,4,2,128]{3,2,1,0:T(2,128)(2,1)} %reshape.95), calls=%async_computation | async-start | bytes 33554432 | tf_op jit(solution)/shard_map/all_to_all | solution.py:108
  575.2 13.7 %multiply_convert_fusion = bf16[4,128,8,512]{3,1,2,0:T(8,128)(2,1)} fusion(bf16[4,8,512,512]{2,3,1,0:T(8,128)(2,1)} %fusion.2, bf16[512,4,64]{2,0,1:T(8,128)(2,1)S(1)} %copy-done.2, bf16[512,4,64]{2,0,1:T(8,128)(2,1)S(1)} %copy-done.1), kind=kOutput, calls=%fused_computation.17 | convolution fusion | flops 2152726528 | bytes 21495808 | tf_op jit(solution)/shard_map/hgqk,khd->qhgd/dot_general | solution.py:52
  599.6 158.1 %all-to-all-done = bf16[8192,4,2,128]{3,2,1,0:T(2,128)(2,1)} async-done(((bf16[8192,4,2,128]{3,2,1,0:T(2,128)(2,1)}), bf16[8192,4,2,128]{3,2,1,0:T(2,128)(2,1)}, u32[]{:S(2)}, u32[]{:S(2)}) %all-to-all-start) | async-done | bytes 16777248 | tf_op jit(solution)/shard_map/all_to_all | solution.py:108
  757.7 15.1 %copy.104 = bf16[8192,4,2,128]{3,0,2,1:T(8,128)(2,1)} copy(bf16[8192,4,2,128]{3,2,1,0:T(2,128)(2,1)} %all-to-all-done) | data formatting | bytes 33554432 | tf_op jit(solution)/shard_map/all_to_all | solution.py:108
  772.9 20.8 %copy.105 = bf16[4096,2,4,2,128]{0,4,3,2,1:T(8,128)(2,1)} copy(bf16[4096,2,4,2,128]{4,0,1,3,2:T(8,128)(2,1)} %bitcast.118) | data formatting | bytes 33554432 | tf_op jit(solution)/shard_map/all_to_all | solution.py:108
  793.7 13.9 %convolution_convert_fusion.2 = bf16[512,4096]{1,0:T(8,128)(2,1)} fusion(bf16[512,2048]{0,1:T(8,128)(2,1)S(1)} %bitcast.125, bf16[4096,2048]{0,1:T(8,128)(2,1)} %bitcast.119), kind=kOutput, calls=%fused_computation.18 | convolution fusion | flops 8592031744 | bytes 23068672 | tf_op jit(solution)/shard_map/dot_general | solution.py:111
  807.5 64.1 %reduce-scatter.2.cloned.1.call-done = bf16[1024,1024]{1,0:T(8,128)(2,1)} async-done(((bf16[16384,1024]{1,0:T(8,128)(2,1)}), bf16[1024,1024]{1,0:T(8,128)(2,1)}) %reduce-scatter.2.cloned.1.call-update) | async-done | bytes 2097168 | tf_op jit(solution)/shard_map/reduce_scatter | solution.py:99
  (41 shorter events, 54.6 us)
Async XLA Ops:
  7.2 18.9 %copy-start.4 = (s32[1,512]{1,0:T(1,128)S(1)}, s32[1,512]{1,0:T(1,128)}, u32[]{:S(2)}) copy-start(s32[1,512]{1,0:T(1,128)} %param.10) | copy-start | bytes 6148
  7.2 174.6 %all-gather.3.cloned.1.call-start = ((), (), s32[]{:S(2)}) async-start(), calls=%async_computation.2 | async-start | bytes 35651584 | tf_op jit(solution)/shard_map/all_gather | solution.py:85
  10.9 585.9 %all-gather.5.cloned.1.call-start = ((), (), s32[]{:S(2)}) async-start(), calls=%async_computation.3 | async-start | bytes 3145728 | tf_op jit(solution)/shard_map/all_gather | solution.py:107
  246.2 34.5 %copy-start.6 = (s32[64]{0:T(128)S(1)}, s32[64]{0:T(128)}, u32[]{:S(2)}) copy-start(s32[64]{0:T(128)} %param.12) | copy-start | bytes 772
  356.3 18.1 %copy-start = (bf16[512,32,128]{0,2,1:T(8,128)(2,1)S(1)}, bf16[512,32,128]{0,2,1:T(8,128)(2,1)}, u32[]{:S(2)}) copy-start(bf16[512,32,128]{0,2,1:T(8,128)(2,1)} %copy.94) | copy-start | bytes 12582916
  417.1 10.1 %copy-start.3 = (bf16[512,4,1,128]{3,0,1,2:T(8,128)(2,1)S(1)}, bf16[512,4,1,128]{3,0,1,2:T(8,128)(2,1)}, u32[]{:S(2)}) copy-start(bf16[512,4,1,128]{3,0,1,2:T(8,128)(2,1)} %convolution_bitcast_fusion) | copy-start | bytes 1572868
  428.3 443.3 %reduce-scatter.2.cloned.1.call-start = ((), (), s32[]{:S(2)}) async-start(), calls=%async_computation.4 | async-start | bytes 35651584 | tf_op jit(solution)/shard_map/reduce_scatter | solution.py:99
  467.6 17.0 %copy-start.5 = (s32[64]{0:T(128)S(1)}, s32[64]{0:T(128)}, u32[]{:S(2)}) copy-start(s32[64]{0:T(128)} %param.13) | copy-start | bytes 772
  562.2 12.9 %copy-start.1 = (bf16[512,4,64]{2,0,1:T(8,128)(2,1)S(1)}, bf16[512,4,64]{2,0,1:T(8,128)(2,1)}, u32[]{:S(2)}) copy-start(bf16[512,4,64]{2,0,1:T(8,128)(2,1)} %get-tuple-element.18) | copy-start | bytes 786436
  562.2 12.9 %copy-start.2 = (bf16[512,4,64]{2,0,1:T(8,128)(2,1)S(1)}, bf16[512,4,64]{2,0,1:T(8,128)(2,1)}, u32[]{:S(2)}) copy-start(bf16[512,4,64]{2,0,1:T(8,128)(2,1)} %get-tuple-element.19) | copy-start | bytes 786436
  562.2 195.5 %all-to-all-start = ((bf16[8192,4,2,128]{3,2,1,0:T(2,128)(2,1)}), bf16[8192,4,2,128]{3,2,1,0:T(2,128)(2,1)}, u32[]{:S(2)}, u32[]{:S(2)}) async-start(bf16[8192,4,2,128]{3,2,1,0:T(2,128)(2,1)} %reshape.95), calls=%async_computation | async-start | bytes 33554432 | tf_op jit(solution)/shard_map/all_to_all | solution.py:108
Sparse Core Ops, SparseCore 0:
  11.0 170.7 all-gather.2
  428.4 33.0 all-gather.4
  541.0 330.5 reduce-scatter.1
where the time goes:
time: 897 us; the launch traced here: 885 us
  waiting for transfers between devices  377 us (42%)
  local copies, waits for them, and re-layouts  287 us (32%)
  matrix products  171 us (19%)
  other arithmetic  22.4 us (2%)
  between operations  14.3 us (2%)
  starting transfers between devices  13 us (1%)
    all_to_all x1, waiting for transfers between devices, local(): lax.all_to_all(weights, 'mp', split_axis=0, concat_axis=1, tiled=True)  158 us
    all_gather x1, waiting for transfers between devices, local(): gathered = lax.all_gather(weight_slots, 'dp', axis=0, tiled=True)  155 us
    all_gather x1, local copies, waits for them, and re-layouts, local(): gathered = lax.all_gather(weight_slots, 'dp', axis=0, tiled=True)  64.4 us
    reduce_scatter x1, waiting for transfers between devices, local(): lax.psum_scatter(term.reshape(slot_rows * lax.axis_size('dp'), head_count...  64.1 us
    all_to_all x2, local copies, waits for them, and re-layouts, local(): lax.all_to_all(weights, 'mp', split_axis=0, concat_axis=1, tiled=True)  36 us
    reshape x1, local copies, waits for them, and re-layouts, pick_blocks(): flat = source.reshape(block_total, -1)  34.5 us
    convert_element_type x1, local copies, waits for them, and re-layouts, local(): term.reshape(slot_rows * lax.axis_size('dp'), head_count * 2 * head_size)  33.2 us
    dot_general x1, matrix products, attend(): prob_grad = jnp.einsum('qhgd,khd->hgqk', outgrad_wide, value_wide)  25.1 us
  transfers between devices with their start and end apart: 4, of which 3 were waited for; matrix products, arithmetic and copies ran while one was open for 25% of the time, Pallas kernels for 0%

commit v1 on v0

v1 whole, which is shorter than its diff:
```python
import functools

import jax
import jax.numpy as jnp
from jax import lax
from jax.experimental import pallas as pl
from jax.experimental.pallas import tpu as pltpu
from jax.sharding import PartitionSpec as P

BR = 128
LOG2E = 1.4426950408889634
VMEM_LIMIT = 60 * 1024 * 1024


def params():
    return pltpu.CompilerParams(
        dimension_semantics=("arbitrary",), vmem_limit_bytes=VMEM_LIMIT
    )


def group_of(count):
    for size in (8, 4, 2):
        if count % size == 0:
            return size
    return 1


def block_specs(group, width):
    return [
        pl.BlockSpec((BR, width), functools.partial(lambda r, i, p: (p[i * group + r], 0), r))
        for r in range(group)
    ]


def project_kernel(group, head_size, place, tok_ref, cos_ref, sin_ref, *refs):
    blocks, out_ref, total = refs[:group], refs[group], refs[group + 1]
    step = pl.program_id(0)

    @pl.when(step == 0)
    def _():
        total[...] = jnp.zeros_like(total)

    w = jnp.concatenate([b[...] for b in blocks], axis=0)
    total[...] += jnp.dot(tok_ref[...], w, preferred_element_type=jnp.float32)

    @pl.when(step == pl.num_programs(0) - 1)
    def _():
        pair = 2 * head_size
        for h in range(total.shape[1] // pair):
            key = total[:, h * pair : h * pair + head_size]
            rot = key * cos_ref[...] + pltpu.roll(key, head_size // 2, 1) * sin_ref[...]
            out_ref[:, h * pair : h * pair + head_size] = rot.astype(jnp.bfloat16)
            value = total[:, h * pair + head_size : (h + 1) * pair]
            out_ref[:, h * pair + head_size : (h + 1) * pair] = value.astype(jnp.bfloat16)


def project(tokens, gathered, place, cos_tab, sin_tab, head_size):
    tok_count = tokens.shape[0]
    width = gathered.shape[1]
    count = place.shape[0]
    group = group_of(count)
    table = pl.BlockSpec((tok_count, head_size), lambda i, p: (0, 0))
    return pl.pallas_call(
        functools.partial(project_kernel, group, head_size),
        out_shape=jax.ShapeDtypeStruct((tok_count, width), jnp.bfloat16),
        grid_spec=pltpu.PrefetchScalarGridSpec(
            num_scalar_prefetch=1,
            grid=(count // group,),
            in_specs=[pl.BlockSpec((tok_count, group * BR), lambda i, p: (0, i)), table, table]
            + block_specs(group, width),
            out_specs=pl.BlockSpec((tok_count, width), lambda i, p: (0, 0)),
            scratch_shapes=[pltpu.VMEM((tok_count, width), jnp.float32)],
        ),
        compiler_params=params(),
        cost_estimate=pl.CostEstimate(
            flops=2 * tok_count * count * BR * width,
            bytes_accessed=2 * (tok_count * count * BR + count * BR * width + tok_count * width),
            transcendentals=0,
        ),
        name="project",
    )(place, tokens, cos_tab, sin_tab, *([gathered] * group))


def attend_kernel(
    per_head, tile, q_ref, og_ref, kv_ref, col_ref, row_ref, cos_ref, sin_ref,
    dq_ref, pair_ref, bias, key_t, rot_acc, val_acc,
):
    tok_count, pair = kv_ref.shape
    hd = pair // 2
    inv_root = 1.0 / (hd ** 0.5)

    @pl.when(pl.program_id(0) == 0)
    def _():
        kpos = lax.broadcasted_iota(jnp.int32, bias.shape, 0)
        qpos = lax.broadcasted_iota(jnp.int32, bias.shape, 1)
        allowed = (kpos <= qpos) & (col_ref[...] == row_ref[...])
        bias[...] = jnp.where(allowed, 0.0, -1e30).astype(jnp.float32)

    key_t[...] = kv_ref[:, :hd].astype(jnp.float32).T.astype(jnp.bfloat16)
    rot_acc[...] = jnp.zeros_like(rot_acc)
    val_acc[...] = jnp.zeros_like(val_acc)

    def head(j, carry):
        lanes = pl.ds(pl.multiple_of(j * hd, hd), hd)
        for t in range(tok_count // tile):
            rows = slice(t * tile, (t + 1) * tile)
            reach = (t + 1) * tile
            q = q_ref[rows, lanes]
            og = og_ref[rows, lanes]
            nt = (((1,), (1,)), ((), ()))
            s = lax.dot_general(kv_ref[:reach, :hd], q, nt, preferred_element_type=jnp.float32)
            s = s * (inv_root * LOG2E) + bias[:reach, rows]
            e = jnp.exp2(s - jnp.max(s, axis=0, keepdims=True))
            p = e * (1.0 / jnp.sum(e, axis=0, keepdims=True))
            pb = p.astype(jnp.bfloat16)
            dp = lax.dot_general(kv_ref[:reach, hd:], og, nt, preferred_element_type=jnp.float32)
            dot = jnp.sum(pb.astype(jnp.float32) * dp, axis=0, keepdims=True)
            ds = (p * (dp - dot)).astype(jnp.bfloat16)
            val_acc[:reach, :] += jnp.dot(pb, og, preferred_element_type=jnp.float32)
            rot_acc[:reach, :] += jnp.dot(ds, q, preferred_element_type=jnp.float32)
            dq = jnp.dot(key_t[:, :reach], ds, preferred_element_type=jnp.float32)
            dq_ref[rows, lanes] = (dq * inv_root).T.astype(jnp.bfloat16)
        return carry

    lax.fori_loop(0, per_head, head, 0, unroll=2)
    g = rot_acc[...] * inv_root
    back = g * cos_ref[...] - pltpu.roll(g, hd // 2, 1) * sin_ref[...]
    pair_ref[:, :hd] = back.astype(jnp.bfloat16)
    pair_ref[:, hd:] = val_acc[...].astype(jnp.bfloat16)


def attend(queries, out_grad, pairs, seg_row, cos_tab, sin_tab, head_count, head_size):
    tok_count, q_width = queries.shape
    per_head = q_width // head_count // head_size
    tile = tok_count // 2 if tok_count % 512 == 0 else tok_count
    slab = pl.BlockSpec((tok_count, per_head * head_size), lambda h: (0, h))
    both = pl.BlockSpec((tok_count, 2 * head_size), lambda h: (0, h))
    table = pl.BlockSpec((tok_count, head_size), lambda h: (0, 0))
    col = pl.BlockSpec((tok_count, 1), lambda h: (0, 0))
    row = pl.BlockSpec((1, tok_count), lambda h: (0, 0))
    return pl.pallas_call(
        functools.partial(attend_kernel, per_head, tile),
        out_shape=(
            jax.ShapeDtypeStruct(queries.shape, jnp.bfloat16),
            jax.ShapeDtypeStruct(pairs.shape, jnp.bfloat16),
        ),
        grid=(head_count,),
        in_specs=[slab, slab, both, col, row, table, table],
        out_specs=(slab, both),
        scratch_shapes=[
            pltpu.VMEM((tok_count, tok_count), jnp.float32),
            pltpu.VMEM((head_size, tok_count), jnp.bfloat16),
            pltpu.VMEM((tok_count, head_size), jnp.float32),
            pltpu.VMEM((tok_count, head_size), jnp.float32),
        ],
        compiler_params=params(),
        cost_estimate=pl.CostEstimate(
            flops=10 * tok_count * tok_count * q_width,
            bytes_accessed=6 * tok_count * q_width + 4 * tok_count * pairs.shape[1],
            transcendentals=tok_count * tok_count * q_width // head_size,
        ),
        name="attend",
    )(queries, out_grad, pairs, seg_row.reshape(-1, 1), seg_row, cos_tab, sin_tab)


def parts_kernel(group, block_of, used, tok_ref, pair_ref, out_ref):
    step = pl.program_id(0)
    for r in range(group):
        slot = step * group + r
        rows = slice(r * BR, (r + 1) * BR)

        @pl.when(used[slot] != 0)
        def _():
            cols = pl.ds(pl.multiple_of(block_of[slot] * BR, BR), BR)
            out_ref[rows, :] = lax.dot_general(
                tok_ref[:, cols], pair_ref[...], (((0,), (0,)), ((), ())),
                preferred_element_type=jnp.float32,
            ).astype(jnp.bfloat16)

        @pl.when(used[slot] == 0)
        def _():
            out_ref[rows, :] = jnp.zeros((BR, out_ref.shape[1]), jnp.bfloat16)


def slot_parts(tokens, pairs, block_of, used):
    slot_total = block_of.shape[0]
    group = group_of(slot_total)
    width = pairs.shape[1]
    return pl.pallas_call(
        functools.partial(parts_kernel, group),
        out_shape=jax.ShapeDtypeStruct((slot_total * BR, width), jnp.bfloat16),
        grid_spec=pltpu.PrefetchScalarGridSpec(
            num_scalar_prefetch=2,
            grid=(slot_total // group,),
            in_specs=[
                pl.BlockSpec(tokens.shape, lambda i, b, u: (0, 0)),
                pl.BlockSpec(pairs.shape, lambda i, b, u: (0, 0)),
            ],
            out_specs=pl.BlockSpec((group * BR, width), lambda i, b, u: (i, 0)),
        ),
        compiler_params=params(),
        cost_estimate=pl.CostEstimate(
            flops=2 * tokens.size * width,
            bytes_accessed=2 * (tokens.size + slot_total * BR * width),
            transcendentals=0,
        ),
        name="slot_parts",
    )(block_of, used, tokens, pairs)


def input_kernel(group, add, place, pair_ref, *refs):
    blocks, out_ref = refs[:group], refs[-1]
    w = jnp.concatenate([b[...] for b in blocks], axis=0)
    total = lax.dot_general(
        pair_ref[...], w, (((1,), (1,)), ((), ())), preferred_element_type=jnp.float32
    )
    if add:
        total = total + refs[group][...].astype(jnp.float32)
    out_ref[...] = total.astype(jnp.bfloat16)


def input_part(pairs, gathered, place, other=None):
    tok_count, width = pairs.shape
    count = place.shape[0]
    group = group_of(count)
    wide = pl.BlockSpec((tok_count, group * BR), lambda i, p: (0, i))
    add = other is not None
    return pl.pallas_call(
        functools.partial(input_kernel, group, add),
        out_shape=jax.ShapeDtypeStruct((tok_count, count * BR), jnp.bfloat16),
        grid_spec=pltpu.PrefetchScalarGridSpec(
            num_scalar_prefetch=1,
            grid=(count // group,),
            in_specs=[pl.BlockSpec(pairs.shape, lambda i, p: (0, 0))]
            + block_specs(group, width)
            + ([wide] if add else []),
            out_specs=wide,
        ),
        compiler_params=params(),
        cost_estimate=pl.CostEstimate(
            flops=2 * tok_count * width * count * BR,
            bytes_accessed=2 * (count * BR * width + 2 * tok_count * count * BR),
            transcendentals=0,
        ),
        name="input_own" if add else "input_other",
    )(place, pairs, *([gathered] * group), *((other,) if add else ()))


def local(tokens, queries, out_grad, segment_ids, weight_slots, old_place, new_place):
    tok_count = tokens.shape[0]
    slot_rows, head_count, _, head_size = weight_slots.shape
    width = head_count * 2 * head_size
    dp_count = lax.axis_size("dp")
    mp_count = lax.axis_size("mp")
    slot_total = dp_count * (slot_rows // BR)
    block_count = old_place.shape[0]

    gathered = lax.all_gather(weight_slots.reshape(slot_rows, width), "dp", axis=0, tiled=True)

    half = head_size // 2
    frequency = 500000.0 ** (-2.0 * jnp.arange(half, dtype=jnp.float32) / head_size)
    angle = jnp.arange(tok_count, dtype=jnp.float32)[:, None] * frequency[None, :]
    cos_half, sin_half = jnp.cos(angle), jnp.sin(angle)
    cos_tab = jnp.concatenate([cos_half, cos_half], axis=1)
    sin_tab = jnp.concatenate([-sin_half, sin_half], axis=1)

    pairs = project(tokens, gathered, old_place, cos_tab, sin_tab, head_size)
    query_grad, pair_grad = attend(
        queries.reshape(tok_count, -1), out_grad.reshape(tok_count, -1), pairs, segment_ids,
        cos_tab, sin_tab, head_count, head_size,
    )

    slot_ids = jnp.arange(slot_total, dtype=jnp.int32)
    matched = (new_place[None, :] == slot_ids[:, None]).astype(jnp.int32)
    block_of = jnp.sum(matched * jnp.arange(block_count, dtype=jnp.int32)[None, :], axis=1)
    used = jnp.sum(matched, axis=1)
    term = slot_parts(tokens, pair_grad, block_of, used)
    term, pair_later, query_grad = lax.optimization_barrier((term, pair_grad, query_grad))
    weight_grad = lax.psum_scatter(term, "dp", scatter_dimension=0, tiled=True)

    me = lax.axis_index("mp")
    share = old_place.reshape(mp_count, block_count // mp_count)
    total = None
    for gap in range(1, mp_count):
        target = lax.rem(me + gap, mp_count)
        places = lax.dynamic_index_in_dim(share, target, 0, keepdims=False)
        piece = input_part(pair_later, gathered, places)
        ring = [(i, (i + gap) % mp_count) for i in range(mp_count)]
        arrived = lax.ppermute(piece, "mp", ring)
        total = arrived if total is None else total + arrived
    mine = lax.dynamic_index_in_dim(share, me, 0, keepdims=False)
    input_grad = input_part(pair_later, gathered, mine, total)
    return (
        input_grad,
        query_grad.reshape(queries.shape),
        weight_grad.astype(jnp.float32).reshape(slot_rows, head_count, 2, head_size),
    )


def solution(mesh):
    return jax.shard_map(
        local,
        mesh=mesh,
        in_specs=(
            P("dp", None),
            P("dp", "mp", None),
            P("dp", "mp", None),
            P("dp", None),
            P("dp", "mp", None, None),
            P(),
            P(),
        ),
        out_specs=(P("dp", "mp"), P("dp", "mp", None), P("dp", "mp", None, None)),
        check_vma=False,
    )
```

time: 897 us -> 618 us (0.69); the launches traced: 885 us -> 617 us
  local copies, waits for them, and re-layouts: 287 us -> 32.8 us
  matrix products: 171 us -> 0 us
  Pallas kernels: 0 us -> 111 us
  waiting for transfers between devices: 377 us -> 455 us
  other arithmetic: 22.4 us -> 2.69 us
  starting transfers between devices: 13 us -> 1.37 us
    all_to_all x1 -> x0, waiting for transfers between devices: 158 us -> none  [local(): lax.all_to_all(weights, 'mp', split_axis=0, concat_axis=1, tiled=True)]
    reduce_scatter x1, waiting for transfers between devices: 64.1 us -> 215 us  [local(): weight_grad = lax.psum_scatter(term, 'dp', scatter_dimension=0, tiled=True)]
    dot_general x10 -> x0, matrix products: 151 us -> none  [the longest x1 25.1 us: attend(): prob_grad = jnp.einsum('qhgd,khd->hgqk', outgrad_wide, value_wide)]
    pallas_call x0 -> x5, Pallas kernels: none -> 111 us  [the longest x1 42.7 us: attend(): pl.pallas_call(functools.partial(attend_kernel, per_head, tile), out_shap...]
    ppermute x0 -> x1, waiting for transfers between devices: none -> 85.2 us  [local(): arrived = lax.ppermute(piece, 'mp', ring)]
    all_gather x2 -> x0, local copies, waits for them, and re-layouts: 67.3 us -> none  [the longest x1 64.4 us: local(): gathered = lax.all_gather(weight_slots, 'dp', axis=0, tiled=True)]
    reshape x5, local copies, waits for them, and re-layouts: 87 us -> 25.2 us  [the longest x1 13.2 us: local(): out_grad.reshape(tok_count, -1)]
    convert_element_type x3 -> x0, local copies, waits for them, and re-layouts: 57.4 us -> none  [the longest x1 33.2 us: local(): term.reshape(slot_rows * lax.axis_size('dp'), head_count * 2 * head_size)]
  transfers between devices with their start and end apart: 4 -> 3, of which waited for: 3 -> 3; matrix products, arithmetic and copies ran while one was open for 25% -> 4% of each run, Pallas kernels for 0% -> 3%
where the time goes in v1:
time: 618 us; the launch traced here: 617 us
  waiting for transfers between devices  455 us (74%)
  Pallas kernels  111 us (18%)
  local copies, waits for them, and re-layouts  32.8 us (5%)
  between operations  14.1 us (2%)
    reduce_scatter x1, waiting for transfers between devices, local(): weight_grad = lax.psum_scatter(term, 'dp', scatter_dimension=0, tiled=True)  215 us
    all_gather x1, waiting for transfers between devices, local(): lax.all_gather(weight_slots.reshape(slot_rows, width), 'dp', axis=0, tile...  154 us
    ppermute x1, waiting for transfers between devices, local(): arrived = lax.ppermute(piece, 'mp', ring)  85.2 us
    pallas_call x1, Pallas kernels, attend(): pl.pallas_call(functools.partial(attend_kernel, per_head, tile), out_shap...  42.7 us
    pallas_call x1, Pallas kernels, slot_parts(): pl.pallas_call(functools.partial(parts_kernel, group), out_shape=jax.Shap...  30.9 us
    pallas_call x2, Pallas kernels, input_part(): pl.pallas_call(functools.partial(input_kernel, group, add), out_shape=jax...  21 us
    pallas_call x1, Pallas kernels, project(): pl.pallas_call(functools.partial(project_kernel, group, head_size), out_s...  16.8 us
    reshape x1, local copies, waits for them, and re-layouts, local(): out_grad.reshape(tok_count, -1)  13.2 us
  transfers between devices with their start and end apart: 3, of which 3 were waited for; matrix products, arithmetic and copies ran while one was open for 4% of the time, Pallas kernels for 3%

profile of v1, /device:TPU:0, one launch (start us, length us, event | category | flops | bytes accessed | tf_op | source)
XLA Modules:
  0.0 617.2 jit_solution(4793941145907442811)
XLA Ops:
  7.2 0.0 all-gather.2.cloned.1.call-start
  7.2 4.4 reshape.39
  11.7 0.0 all-gather.2.cloned.1.call-update
  11.7 0.0 reduce-scatter.2.cloned.1.call-start
  11.7 0.9 copy.11.col_ref
  12.6 0.7 convert_reduce_fusion
  13.3 1.0 fusion.2
  14.3 1.0 pad_maximum_fusion
  15.3 13.2 %copy_bitcast_fusion = (bf16[512,4096]{1,0:T(8,128)(2,1)}, bf16[512,4096]{1,0:T(8,128)(2,1)}) fusion(bf16[64,8,32,128]{3,2,1,0:T(8,128)(2,1)} %bitcast.15, bf16[64,8,32,128]{3,2,1,0:T(8,128)(2,1)} %bitcast.16), kind=kLoop, calls=%fused_computation | loop fusion | bytes 16777216 | tf_op jit(solution)/shard_map/reshape | solution.py:269
  28.5 154.1 %all-gather.2.cloned.1.call-done.refs_0_.refs_1_.refs_2_.refs_3_.refs_4_.refs_5_.refs_6_.refs_7_ = bf16[16384,1024]{1,0:T(8,128)(2,1)} async-done(((bf16[1024,1024]{1,0:T(8,128)(2,1)}), bf16[16384,1024]{1,0:T(8,128)(2,1)}) %all-gather.2.cloned.1.call-update) | async-done | bytes 33554448 | tf_op jit(solution)/shard_map/all_gather | solution.py:258
  182.6 16.8 %project.1.kv_ref = bf16[512,1024]{1,0:T(8,128)(2,1)} custom-call(s32[64]{0:T(128)} %place.1, bf16[512,8192]{1,0:T(8,128)(2,1)} %tok_ref.3, f32[512,128]{1,0:T(8,128)} %get-tuple-element.20.cos_ref, f32[512,128]{1,0:T(8,128)} %get-tuple-element.21.sin_ref, ...), custom_call_target="tpu_custom_call" | custom-call | flops 8589934592 | bytes 26214400 | tf_op jit(solution)/shard_map/project/pallas_call | solution.py:63
  199.4 42.7 %attend.1 = (bf16[512,4096]{1,0:T(8,128)(2,1)}, bf16[512,1024]{1,0:T(8,128)(2,1)}) custom-call(bf16[512,4096]{1,0:T(8,128)(2,1)} %get-tuple-element.23.q_ref, bf16[512,4096]{1,0:T(8,128)(2,1)} %get-tuple-element.22.og_ref, bf16[512,1024]{1,0:T(8,128)(2,1)} %project.1.kv_ref, s32[512,1]{1,0:T(8,128)} %copy.11.col_ref, s32[1,512]{1,0:T(1,128)} %row_ref.1, ...), custom_call_target="tpu_custom_call" | custom-call | flops 10737418240 | bytes 14680064 | tf_op jit(solution)/shard_map/attend/pallas_call | solution.py:141
  242.1 30.9 %slot_parts.1 = bf16[16384,1024]{1,0:T(8,128)(2,1)} custom-call(s32[128]{0:T(128)} %get-tuple-element.14.block_of, s32[128]{0:T(128)} %get-tuple-element.13.used, bf16[512,8192]{1,0:T(8,128)(2,1)} %tok_ref.3, bf16[512,1024]{1,0:T(8,128)(2,1)} %get-tuple-element.10.pair_ref), custom_call_target="tpu_custom_call" | custom-call | flops 8589934592 | bytes 41943040 | tf_op jit(solution)/shard_map/slot_parts/pallas_call | solution.py:189
  273.0 0.0 reduce-scatter.2.cloned.1.call-update
  273.0 0.6 copy-done.1
  273.6 0.1 reshape.36
  273.7 0.5 dynamic-slice_bitcast_fusion
  274.3 10.2 %input_other.1 = bf16[512,4096]{1,0:T(8,128)(2,1)} custom-call(s32[32]{0:T(128)} %get-tuple-element.15.place, bf16[512,1024]{1,0:T(8,128)(2,1)} %get-tuple-element.10.pair_ref, bf16[16384,1024]{1,0:T(8,128)(2,1)} %all-gather.2.cloned.1.call-done.refs_0_.refs_1_.refs_2_.refs_3_.refs_4_.refs_5_.refs_6_.refs_7_, ...), custom_call_target="tpu_custom_call" | custom-call | flops 4294967296 | bytes 16777216 | tf_op jit(solution)/shard_map/input_other/pallas_call | solution.py:228
  284.5 1.3 collective-permute-start
  285.8 6.5 %copy.14 = bf16[64,8,32,128]{3,2,1,0:T(8,128)(2,1)} copy(bf16[64,8,32,128]{3,1,2,0:T(8,128)(2,1)} %bitcast.13) | data formatting | bytes 8388608
  292.3 85.2 %collective-permute-done.refs_8_ = bf16[512,4096]{1,0:T(8,128)(2,1)} collective-permute-done((bf16[512,4096]{1,0:T(8,128)(2,1)}, bf16[512,4096]{1,0:T(8,128)(2,1)}, u32[]{:S(2)}, u32[]{:S(2)}) %collective-permute-start) | collective-permute-done | bytes 4194336 | tf_op jit(solution)/shard_map/ppermute | solution.py:289
  377.5 10.8 %input_own.1 = bf16[512,4096]{1,0:T(8,128)(2,1)} custom-call(s32[32]{0:T(128)} %get-tuple-element.16.place, bf16[512,1024]{1,0:T(8,128)(2,1)} %get-tuple-element.10.pair_ref, bf16[16384,1024]{1,0:T(8,128)(2,1)} %all-gather.2.cloned.1.call-done.refs_0_.refs_1_.refs_2_.refs_3_.refs_4_.refs_5_.refs_6_.refs_7_, ...), custom_call_target="tpu_custom_call" | custom-call | flops 4294967296 | bytes 16777216 | tf_op jit(solution)/shard_map/input_own/pallas_call | solution.py:228
  388.3 215.5 %reduce-scatter.2.cloned.1.call-done = bf16[1024,1024]{1,0:T(8,128)(2,1)} async-done(((bf16[16384,1024]{1,0:T(8,128)(2,1)}), bf16[1024,1024]{1,0:T(8,128)(2,1)}) %reduce-scatter.2.cloned.1.call-update) | async-done | bytes 2097168 | tf_op jit(solution)/shard_map/reduce_scatter | solution.py:279
  603.7 6.6 %reshape.45 = f32[1024,4,2,128]{3,2,1,0:T(2,128)} reshape(bf16[1024,1024]{1,0:T(8,128)(2,1)} %reduce-scatter.2.cloned.1.call-done) | data formatting | bytes 6291456 | tf_op jit(solution)/shard_map/reshape | solution.py:296
  (6 shorter events, 0.0 us)
Async XLA Ops:
  7.2 4.6 copy-start
  7.2 5.4 copy-start.2
  7.2 175.4 %all-gather.2.cloned.1.call-start = ((), (), s32[]{:S(2)}) async-start(), calls=%async_computation.1 | async-start | bytes 35651584 | tf_op jit(solution)/shard_map/all_gather | solution.py:258
  11.7 592.1 %reduce-scatter.2.cloned.1.call-start = ((), (), s32[]{:S(2)}) async-start(), calls=%async_computation.2 | async-start | bytes 35651584 | tf_op jit(solution)/shard_map/reduce_scatter | solution.py:279
  273.0 0.7 copy-start.1
  284.5 93.0 %collective-permute-start = (bf16[512,4096]{1,0:T(8,128)(2,1)}, bf16[512,4096]{1,0:T(8,128)(2,1)}, u32[]{:S(2)}, u32[]{:S(2)}) collective-permute-start(bf16[512,4096]{1,0:T(8,128)(2,1)} %input_other.1), channel_id=1, source_target_pairs={{0,1},{1,0},{2,3},{3,2},{4,5},{5,4},{6,7},{7,6},{8,9},{9,8},{10,11... | collective-permute-start | bytes 12582920 | tf_op jit(solution)/shard_map/ppermute | solution.py:289
Sparse Core Ops, SparseCore 0:
  11.8 170.7 all-gather.1
  273.1 330.5 reduce-scatter.1
